TPU v7x, 32 devices: a whole 2x2x4 slice. The times are simulated.
32 devices in a mesh: dp: 8 (over z, x), mp: 4 (over y, core).
Axes of the slice: x: 2, y: 2, z: 4, core: 2. Of those that a mesh axis runs over, the one named last changes fastest.
Arguments:
- patches: bfloat16 [4096, 2048], P('dp'), may hold values from -6 to 6
- cotangent: bfloat16 [4096, 8192], P('dp', 'mp'), may hold values from -0.09375 to 0.09375
- weight: float32 [2048, 8192], P('dp', 'mp'), may hold values from -0.125 to 0.125
- accum: float32 [2048, 8192], P('dp', 'mp'), may hold values from 0.1 to 4
Outputs:
- new_weight: float32 [2048, 8192], P(('dp', 'mp'))
- new_accum: float32 [2048, 8192], P(('dp', 'mp'))
- weight_copy: bfloat16 [2048, 8192], P(None, 'mp')
All inputs are finite; a program needn't handle non-finite values.
Results may differ from a plain program's by a relative error of at most 0.001.
Values may be sent and summed in bfloat16 or wider, within the bound.
A program may use at most 192 MiB of HBM per device.

v0:
```python
import functools

import jax
import jax.numpy as jnp
from jax import lax
from jax.experimental import pallas as pl
from jax.experimental.pallas import tpu as pltpu
from jax.sharding import PartitionSpec as P

learning_rate = 0.02
chunks = 8


def kernel(a, b, m, direct, p_ref, t_ref, w_ref, s_ref, ow_ref, os_ref, oc_ref,
           pv, tv, wv, sv, cv, rbuf, sbuf,
           psem, tsem, lsem, rsend, rrecv, csend, crecv, xsend, xrecv, msend, mrecv, osem):
    nc, _, tok, cc = tv.shape
    rows, full = w_ref.shape
    sub = rows // m
    me = lax.axis_index("dp")
    mi = lax.axis_index("mp")
    zi = lax.div(me, b)
    xi = lax.rem(me, b)
    has_left = zi > 0
    has_right = zi < a - 1

    def inner(j):
        return lax.rem(xi + j, b)

    def peer(j):
        return {"dp": zi * b + inner(j)}

    def other(j):
        return lax.rem(mi + j, m)

    left, right = {"dp": me - b}, {"dp": me + b}

    def remote(src, dst, send, recv, device):
        return pltpu.make_async_remote_copy(
            src_ref=src, dst_ref=dst, send_sem=send, recv_sem=recv,
            device_id=device, device_id_type=pl.DeviceIdType.MESH)

    def cols(c):
        return pl.ds(pl.multiple_of(c * cc, cc), cc)

    def block(i):
        return pl.ds(pl.multiple_of(i * rows, rows), rows)

    def features(i):
        return p_ref.at[:, block(i)] if direct else p_ref.at[block(i)]

    def own_tokens(c):
        return pltpu.make_async_copy(t_ref.at[:, cols(c)], tv.at[c, xi], lsem.at[0, c])

    def own_weight(c):
        return pltpu.make_async_copy(w_ref.at[:, cols(c)], wv.at[c], lsem.at[1, c])

    def own_accum(c):
        return pltpu.make_async_copy(s_ref.at[:, cols(c)], sv.at[c], lsem.at[2, c])

    def own_features(d):
        return pltpu.make_async_copy(features(d * b + xi), pv.at[d, xi], psem.at[2, d, 0])

    def send_tokens(c, j):
        return remote(t_ref.at[:, cols(c)], tv.at[c, xi], tsem.at[0, c, j], tsem.at[1, c, j], peer(j))

    def recv_tokens(c, j):
        return remote(t_ref.at[:, cols(c)], tv.at[c, inner(b - j)], tsem.at[0, c, j], tsem.at[1, c, j], peer(j))

    def send_features(d, j):
        return remote(features(d * b + inner(j)), pv.at[d, xi], psem.at[0, d, j], psem.at[1, d, j], peer(j))

    def recv_features(d, j):
        return remote(features(d * b + xi), pv.at[d, inner(b - j)], psem.at[0, d, j], psem.at[1, d, j], peer(j))

    def pass_sum(side, c, d):
        return remote(sbuf.at[c, d], rbuf.at[side, c, d], rsend.at[c, d], rrecv.at[side, c, d],
                      right if side == 0 else left)

    def region(owner, c):
        return oc_ref.at[block(owner), cols(c)]

    def pass_copy(side, c, h, owner, src=None):
        return remote(region(owner, c) if src is None else src, region(owner, c),
                      csend.at[side, c, h], crecv.at[side, c, h], right if side == 0 else left)

    def share_copy(c, z, j, src=None):
        owner = z * b + xi
        return remote(region(owner, c) if src is None else src, region(owner, c),
                      xsend.at[c, z, j], xrecv.at[c, z, j], peer(j))

    def recv_share(c, z, j):
        spot = region(z * b + inner(b - j), c)
        return remote(spot, spot, xsend.at[c, z, j], xrecv.at[c, z, j], peer(j))

    def flat(c, k, src_dev):
        ref = ow_ref if k == 0 else os_ref
        start = pl.multiple_of(src_dev * full + c * cc, cc)
        return ref.at[:, pl.ds(start, cc)]

    def part(c, k, i):
        v = wv if k == 0 else sv
        return v.at[c, pl.ds(pl.multiple_of(i * sub, sub), sub)]

    def send_flat(c, k, j):
        return remote(part(c, k, other(j)), flat(c, k, mi), msend.at[c, k, j], mrecv.at[c, k, j], {"mp": other(j)})

    def recv_flat(c, k, j):
        return remote(part(c, k, mi), flat(c, k, other(m - j)), msend.at[c, k, j], mrecv.at[c, k, j], {"mp": other(j)})

    def own_flat(c, k):
        return pltpu.make_async_copy(part(c, k, mi), flat(c, k, mi), osem.at[c, k])

    def own_copy(c):
        return pltpu.make_async_copy(cv.at[c], region(me, c), osem.at[c, 2])

    barrier = pltpu.get_barrier_semaphore()

    def greet(device):
        pl.semaphore_signal(barrier, inc=1, device_id=device, device_id_type=pl.DeviceIdType.MESH)

    for d in range(a):
        own_features(d).start()

    @pl.loop(0, nc)
    def _(c):
        own_tokens(c).start()
        own_weight(c).start()
        own_accum(c).start()

    for j in range(1, b):
        greet(peer(j))
    for j in range(1, m):
        greet({"mp": other(j)})
    pl.when(has_left)(lambda: greet(left))
    pl.when(has_right)(lambda: greet(right))
    pl.semaphore_wait(barrier, b - 1 + m - 1 + jnp.minimum(zi, 1) + jnp.minimum(a - 1 - zi, 1))

    for j in range(1, b):
        send_tokens(0, j).start()
    def in_order(do):
        for k in range(a):
            pl.when(a - 1 - k > zi)(functools.partial(do, 0, a - 1 - k))
            pl.when(k < zi)(functools.partial(do, 1, k))

    def start_features(_, d):
        for j in range(1, b):
            send_features(d, j).start()

    in_order(start_features)
    start_features(0, zi)

    @pl.loop(1, nc)
    def _(c):
        for j in range(1, b):
            send_tokens(c, j).start()

    def product(p, t):
        return lax.dot_general(p, t, (((0 if direct else 1,), (0,)), ((), ())), preferred_element_type=jnp.float32)

    def partial(c, d):
        total = product(pv[d, 0], tv[c, 0])
        for x in range(1, b):
            total += product(pv[d, x], tv[c, x])
        return total

    def features_here(d):
        own_features(d).wait()
        for j in range(1, b):
            recv_features(d, j).wait_recv()

    def stage_sums(c):
        own_tokens(c).wait()
        for j in range(1, b):
            recv_tokens(c, j).wait_recv()

        def step(side, d):
            pl.when(c == 0)(lambda: features_here(d))
            sbuf[c, d] = partial(c, d)

            @pl.when(has_left if side == 0 else has_right)
            def _():
                pass_sum(side, c, d).wait_recv()
                sbuf[c, d] += rbuf[side, c, d]

            pass_sum(side, c, d).start()

        in_order(step)

    def stage_update(c):
        pl.when(c == 0)(lambda: features_here(zi))
        own_weight(c).wait()
        own_accum(c).wait()
        sbuf[c, zi] = partial(c, zi)
        for side, there in ((0, has_left), (1, has_right)):
            @pl.when(there)
            def _(side=side):
                pass_sum(side, c, zi).wait_recv()
                sbuf[c, zi] += rbuf[side, c, zi]
        grad = sbuf[c, zi]
        summed = sv[c] + grad * grad
        weight = wv[c] - learning_rate * grad * lax.rsqrt(summed)
        sv[c] = summed
        wv[c] = weight
        cv[c] = weight.astype(cv.dtype)
        pl.when(has_right)(lambda: pass_copy(0, c, 0, me, cv.at[c]).start())
        pl.when(has_left)(lambda: pass_copy(1, c, 0, me, cv.at[c]).start())
        for j in range(1, b):
            share_copy(c, zi, j, cv.at[c]).start()
        own_copy(c).start()
        for k in range(2):
            for j in range(1, m):
                send_flat(c, k, j).start()
            own_flat(c, k).start()

    def stage_forward(h, c):
        def hop(side):
            owner_z = zi - h if side == 0 else zi + h
            owner = owner_z * b + xi
            pass_copy(side, c, h - 1, owner).wait_recv()
            pl.when(has_right if side == 0 else has_left)(
                lambda: pass_copy(side, c, h, owner).start())
            for j in range(1, b):
                share_copy(c, owner_z, j).start()

        pl.when(zi >= h)(functools.partial(hop, 0))
        pl.when(zi + h < a)(functools.partial(hop, 1))

    @pl.loop(0, nc + a)
    def _(i):
        pl.when(i < nc)(lambda: stage_sums(i))
        pl.when((i >= 1) & (i - 1 < nc))(lambda: stage_update(i - 1))
        for h in range(1, a):
            pl.when((i >= 1 + h) & (i - 1 - h < nc))(lambda h=h: stage_forward(h, i - 1 - h))

    for d in range(a):
        for j in range(1, b):
            send_features(d, j).wait_send()

    @pl.loop(0, nc)
    def _(c):
        for j in range(1, b):
            send_tokens(c, j).wait_send()
            for z in range(a):
                share_copy(c, z, j).wait_send()
                recv_share(c, z, j).wait_recv()
        for d in range(a):
            pl.when(d != zi)(lambda d=d: pass_sum(0, c, d).wait_send())
        for h in range(a - 1):
            pl.when((zi >= h) & has_right)(lambda h=h: pass_copy(0, c, h, me).wait_send())
            pl.when((zi + h < a) & has_left)(lambda h=h: pass_copy(1, c, h, me).wait_send())
        own_copy(c).wait()
        for k in range(2):
            for j in range(1, m):
                send_flat(c, k, j).wait_send()
                recv_flat(c, k, j).wait_recv()
            own_flat(c, k).wait()


def shards(n, m, patches, cotangent, weight, accum):
    a = 1
    while a * a < n:
        a *= 2
    b = n // a
    nc = chunks
    direct = weight.shape[0] % 128 == 0
    tok, dim = patches.shape
    rows, full = weight.shape
    cc = full // nc
    f32, bf16 = jnp.float32, jnp.bfloat16
    dma = pltpu.SemaphoreType.DMA
    flops = 2 * tok * b * a * rows * full
    return pl.pallas_call(
        functools.partial(kernel, a, b, m, direct),
        out_shape=(
            pltpu.VMEM((rows // m, full * m), f32),
            pltpu.VMEM((rows // m, full * m), f32),
            pltpu.VMEM((dim, full), bf16),
        ),
        in_specs=[pl.BlockSpec(memory_space=pl.ANY)] * 4,
        out_specs=(pl.BlockSpec(memory_space=pltpu.VMEM),) * 3,
        scratch_shapes=[
            pltpu.VMEM((a, b, tok, rows) if direct else (a, b, rows, tok), bf16),
            pltpu.VMEM((nc, b, tok, cc), bf16),
            pltpu.VMEM((nc, rows, cc), f32),
            pltpu.VMEM((nc, rows, cc), f32),
            pltpu.VMEM((nc, rows, cc), bf16),
            pltpu.VMEM((2, nc, a, rows, cc), f32),
            pltpu.VMEM((nc, a, rows, cc), f32),
            dma((3, a, b)),
            dma((2, nc, b)),
            dma((3, nc)),
            dma((nc, a)),
            dma((2, nc, a)),
            dma((2, nc, a)),
            dma((2, nc, a)),
            dma((nc, a, b)),
            dma((nc, a, b)),
            dma((nc, 2, m)),
            dma((nc, 2, m)),
            dma((nc, 3)),
        ],
        compiler_params=pltpu.CompilerParams(
            collective_id=0, has_side_effects=True, vmem_limit_bytes=42 * 1024 * 1024),
        cost_estimate=pl.CostEstimate(flops=flops, bytes_accessed=4 * dim * full, transcendentals=rows * full),
    )(patches if direct else patches.T, cotangent, weight, accum)


def solution(mesh):
    return jax.shard_map(
        functools.partial(shards, mesh.shape["dp"], mesh.shape["mp"]),
        mesh=mesh,
        in_specs=(P("dp", None), P("dp", "mp"), P("dp", "mp"), P("dp", "mp")),
        out_specs=(P(("dp", "mp"), None), P(("dp", "mp"), None), P(None, "mp")),
        check_vma=False,
    )
```

profile of v0, /device:TPU:0, one launch (start us, length us, event | category | flops | bytes accessed | tf_op | source)
XLA Modules:
  0.0 223.8 jit_solution(7927745257077757391)
XLA Ops:
  0.6 217.2 %shard_map.67 = (f32[64,8192]{1,0:T(8,128)S(1)}, f32[64,8192]{1,0:T(8,128)S(1)}, bf16[2048,2048]{1,0:T(8,128)(2,1)S(1)}) custom-call(bf16[512,2048]{1,0:T(8,128)(2,1)} %p_ref.1, bf16[512,2048]{1,0:T(8,128)(2,1)} %t_ref.1, f32[256,2048]{1,0:T(8,128)} %w_ref.1, f32[256,2048]{1,0:T(8,128)} %s_ref.1), custom_call_target="tpu_custom_call" | custom-call | flops 4294967296 | bytes 16777216 | tf_op jit(solution)/shard_map/pallas_call | solution.py:273
  217.8 1.3 copy.10
  219.1 1.3 copy.11
  220.4 3.4 %copy.12 = bf16[2048,2048]{1,0:T(8,128)(2,1)} copy(bf16[2048,2048]{1,0:T(8,128)(2,1)S(1)} %get-tuple-element.5) | data formatting | bytes 16777216
where the time goes:
time: 224 us
  Pallas kernels  217 us (97%)
  local copies, waits for them, and re-layouts  6.04 us (3%)
    pallas_call x1, Pallas kernels, shards(): pl.pallas_call(functools.partial(kernel, a, b, m, direct), out_shape=(plt...  217 us
    unnamed x3, local copies, waits for them, and re-layouts  6.04 us

commit v1 on v0

v1 whole, which is shorter than its diff:
```python
import functools

import jax
import jax.numpy as jnp
from jax import lax
from jax.experimental import pallas as pl
from jax.experimental.pallas import tpu as pltpu
from jax.sharding import PartitionSpec as P

learning_rate = 0.02
largest_product = 0.5625
power = 7
lag = 1


def kernel(a, b, m, direct, wide, scale, p_ref, t_ref, w_ref, s_ref, ow_ref, os_ref, oc_ref,
           pv, pt, tv, wv, sv, cv, gv, rbuf, sbuf,
           fown, fsend, frecv, qsend, qrecv, tsem, lsem, rsend, rrecv, csend, crecv, xsend, xrecv, msend, mrecv, osem):
    nc, _, cc = tv.shape
    rows, full = w_ref.shape
    tok = tv.shape[1] // b
    part_tok = tok // m
    sub = rows // m
    me = lax.axis_index("dp")
    mi = lax.axis_index("mp")
    zi = lax.div(me, b)
    xi = lax.rem(me, b)
    has_left = zi > 0
    has_right = zi < a - 1

    def inner(j):
        return lax.rem(xi + j, b)

    def peer(j):
        return {"dp": zi * b + inner(j)}

    def other(j):
        return lax.rem(mi + j, m)

    left, right = {"dp": me - b}, {"dp": me + b}

    def remote(src, dst, send, recv, device):
        return pltpu.make_async_remote_copy(
            src_ref=src, dst_ref=dst, send_sem=send, recv_sem=recv,
            device_id=device, device_id_type=pl.DeviceIdType.MESH)

    def cols(c):
        return pl.ds(pl.multiple_of(c * cc, cc), cc)

    def block(i):
        return pl.ds(pl.multiple_of(i * rows, rows), rows)

    def span(start, size):
        return pl.ds(pl.multiple_of(start, size), size)

    def features(i, q=None):
        toks = slice(None) if q is None else span(q * part_tok, part_tok)
        return p_ref.at[toks, block(i)] if direct else p_ref.at[block(i), toks]

    def gathered(d, x, q=None):
        if direct:
            return pv.at[d, x] if q is None else pv.at[d, x, span(q * part_tok, part_tok)]
        return pt.at[d, :, span(x * tok, tok)] if q is None else pt.at[d, :, span(x * tok + q * part_tok, part_tok)]

    def own_features(d):
        return pltpu.make_async_copy(features(d * b + xi), gathered(d, xi), fown.at[d])

    def send_features(d, j):
        return remote(features(d * b + inner(j), mi), gathered(d, xi, mi), fsend.at[d, j], frecv.at[d, j], peer(j))

    def recv_features(d, j):
        return remote(features(d * b + xi, mi), gathered(d, inner(b - j), mi), fsend.at[d, j], frecv.at[d, j], peer(j))

    def relay_features(d, j, k):
        spot = gathered(d, inner(b - j), mi)
        return remote(spot, spot, qsend.at[d, j, k], qrecv.at[d, j, k], {"mp": other(k)})

    def recv_relay(d, j, k):
        spot = gathered(d, inner(b - j), other(m - k))
        return remote(spot, spot, qsend.at[d, j, k], qrecv.at[d, j, k], {"mp": other(k)})

    def tokens_at(c, x):
        return tv.at[c, span(x * tok, tok)]

    def own_tokens(c):
        return pltpu.make_async_copy(t_ref.at[:, cols(c)], tokens_at(c, xi), lsem.at[0, c])

    def own_weight(c):
        return pltpu.make_async_copy(w_ref.at[:, cols(c)], wv.at[c], lsem.at[1, c])

    def own_accum(c):
        return pltpu.make_async_copy(s_ref.at[:, cols(c)], sv.at[c], lsem.at[2, c])

    def send_tokens(c, j):
        return remote(t_ref.at[:, cols(c)], tokens_at(c, xi), tsem.at[0, c, j], tsem.at[1, c, j], peer(j))

    def recv_tokens(c, j):
        return remote(t_ref.at[:, cols(c)], tokens_at(c, inner(b - j)), tsem.at[0, c, j], tsem.at[1, c, j], peer(j))

    def pass_sum(side, c, d):
        return remote(sbuf.at[c, d], rbuf.at[side, c, d], rsend.at[c, d], rrecv.at[side, c, d],
                      right if side == 0 else left)

    def region(owner, c):
        return oc_ref.at[block(owner), cols(c)]

    def pass_copy(side, c, h, owner_z, j, src=None):
        spot = region(owner_z * b + inner(j), c)
        return remote(spot if src is None else src, spot, csend.at[side, c, h, j], crecv.at[side, c, h, j],
                      right if side == 0 else left)

    def share_copy(c, z, j, src=None):
        spot = region(z * b + xi, c)
        return remote(spot if src is None else src, spot, xsend.at[c, z, j], xrecv.at[c, z, j], peer(j))

    def recv_share(c, z, j):
        spot = region(z * b + inner(b - j), c)
        return remote(spot, spot, xsend.at[c, z, j], xrecv.at[c, z, j], peer(j))

    def flat(c, k, src_dev):
        ref = ow_ref if k == 0 else os_ref
        return ref.at[:, span(src_dev * full + c * cc, cc)]

    def part(c, k, i):
        v = wv if k == 0 else sv
        return v.at[c, span(i * sub, sub)]

    def send_flat(c, k, j):
        return remote(part(c, k, other(j)), flat(c, k, mi), msend.at[c, k, j], mrecv.at[c, k, j], {"mp": other(j)})

    def recv_flat(c, k, j):
        return remote(part(c, k, mi), flat(c, k, other(m - j)), msend.at[c, k, j], mrecv.at[c, k, j], {"mp": other(j)})

    def own_flat(c, k):
        return pltpu.make_async_copy(part(c, k, mi), flat(c, k, mi), osem.at[c, k])

    def own_copy(c):
        return pltpu.make_async_copy(cv.at[c], region(me, c), osem.at[c, 2])

    def across_first(c):
        return lax.rem(c * wide, 16) >= 16 - wide

    def valid(c):
        return (c >= 0) & (c < nc)

    barrier = pltpu.get_barrier_semaphore()

    def greet(device):
        pl.semaphore_signal(barrier, inc=1, device_id=device, device_id_type=pl.DeviceIdType.MESH)

    for j in range(1, b):
        greet(peer(j))
    for j in range(1, m):
        greet({"mp": other(j)})
    pl.when(has_left)(lambda: greet(left))
    pl.when(has_right)(lambda: greet(right))

    for d in range(a):
        own_features(d).start()

    @pl.loop(0, nc)
    def _(c):
        own_tokens(c).start()
        own_weight(c).start()
        own_accum(c).start()

    pl.semaphore_wait(barrier, b - 1 + m - 1 + jnp.minimum(zi, 1) + jnp.minimum(a - 1 - zi, 1))

    def in_order(do):
        for k in range(a):
            pl.when(a - 1 - k > zi)(functools.partial(do, a - 1 - k))
            pl.when(k < zi)(functools.partial(do, k))
        do(zi)

    def start_features(d):
        for j in range(1, b):
            send_features(d, j).start()

    for j in range(1, b):
        send_tokens(0, j).start()
    in_order(start_features)

    @pl.loop(1, nc)
    def _(c):
        for j in range(1, b):
            send_tokens(c, j).start()

    def spread_features(d):
        for j in range(1, b):
            recv_features(d, j).wait_recv()
            for k in range(1, m):
                relay_features(d, j, k).start()

    in_order(spread_features)

    def product(c, d):
        return jnp.dot(pt[d], tv[c], preferred_element_type=jnp.float32)

    def coded(v):
        v = v * scale
        square = v * v
        return (square * square * square * v).astype(jnp.bfloat16)

    def decoded(code):
        c = code.astype(jnp.float32)
        size = jnp.maximum(jnp.abs(c), 2.0 ** -126)
        return c * jnp.exp2(jnp.log2(size) * (1 / power - 1)) * (1 / scale)

    def features_here(d):
        own_features(d).wait()
        for j in range(1, b):
            for k in range(1, m):
                recv_relay(d, j, k).wait_recv()
        if direct:
            for x in range(b):
                pt[d, :, x * tok:(x + 1) * tok] = pv[d, x].T

    def stage_tokens(c):
        own_tokens(c).wait()
        for j in range(1, b):
            recv_tokens(c, j).wait_recv()

    def stage_sums(side, c):
        count, fed = (a - 1 - zi, has_left) if side == 0 else (zi, has_right)

        @pl.loop(0, count)
        def _(k):
            d = a - 1 - k if side == 0 else k
            pl.when(c == 0)(lambda: features_here(d))

            @pl.when(fed)
            def _():
                total = product(c, d)
                pass_sum(side, c, d).wait_recv()
                sbuf[c, d] = coded(total + decoded(rbuf[side, c, d]))

            @pl.when(jnp.logical_not(fed))
            def _():
                sbuf[c, d] = coded(product(c, d))

            pass_sum(side, c, d).start()

    def stage_update(c):
        pl.when(c == 0)(lambda: features_here(zi))
        gv[...] = product(c, zi)
        for side, there in ((0, has_left), (1, has_right)):
            @pl.when(there)
            def _(side=side):
                pass_sum(side, c, zi).wait_recv()
                gv[...] += decoded(rbuf[side, c, zi])
        own_weight(c).wait()
        own_accum(c).wait()
        grad = gv[...]
        summed = sv[c] + grad * grad
        weight = wv[c] - learning_rate * grad * lax.rsqrt(summed)
        cv[c] = weight.astype(cv.dtype)
        sv[c] = summed
        wv[c] = weight
        pl.when(has_right)(lambda: pass_copy(0, c, 0, zi, 0, cv.at[c]).start())
        pl.when(has_left)(lambda: pass_copy(1, c, 0, zi, 0, cv.at[c]).start())
        for j in range(1, b):
            share_copy(c, zi, j, cv.at[c]).start()
        own_copy(c).start()
        for k in range(2):
            for j in range(1, m):
                send_flat(c, k, j).start()
            own_flat(c, k).start()

    def stage_across(c):
        for j in range(1, b):
            recv_share(c, zi, b - j).wait_recv()
            pl.when(has_right)(lambda: pass_copy(0, c, 0, zi, j).start())
            pl.when(has_left)(lambda: pass_copy(1, c, 0, zi, j).start())

    def distance(z):
        return jnp.maximum(z, a - 1 - z) * lag

    @pl.loop(0, nc + (2 * (a - 1) + 1) * lag)
    def _(i):
        ready = i - jnp.minimum(zi, a - 1 - zi) * lag
        pl.when(valid(ready))(lambda: stage_tokens(ready))
        going_right = i - zi * lag
        pl.when(valid(going_right))(lambda: stage_sums(0, going_right))
        going_left = i - (a - 1 - zi) * lag
        pl.when(valid(going_left))(lambda: stage_sums(1, going_left))
        mine = i - distance(zi)
        pl.when(valid(mine))(lambda: stage_update(mine))
        if wide:
            before = mine - lag
            pl.when(valid(before) & across_first(before))(lambda: stage_across(before))
        for h in range(1, a):
            for side in range(2):
                owner_z = zi - h if side == 0 else zi + h
                there = owner_z >= 0 if side == 0 else owner_z < a
                further = has_right if side == 0 else has_left
                c = i - distance(owner_z) - h * lag

                @pl.when(there & valid(c))
                def _(side=side, h=h, c=c, owner_z=owner_z, further=further):
                    pass_copy(side, c, h - 1, owner_z, 0).wait_recv()
                    pl.when(further)(lambda: pass_copy(side, c, h, owner_z, 0).start())

                    @pl.when(jnp.logical_not(across_first(c)))
                    def _():
                        for j in range(1, b):
                            share_copy(c, owner_z, j).start()

                if wide:
                    e = c - lag

                    @pl.when(there & valid(e) & across_first(e))
                    def _(side=side, h=h, e=e, owner_z=owner_z, further=further):
                        for j in range(1, b):
                            pass_copy(side, e, h - 1, owner_z, j).wait_recv()
                            pl.when(further)(lambda: pass_copy(side, e, h, owner_z, j).start())

    for d in range(a):
        for j in range(1, b):
            send_features(d, j).wait_send()
            for k in range(1, m):
                relay_features(d, j, k).wait_send()

    @pl.loop(0, nc)
    def _(c):
        straight = jnp.logical_not(across_first(c))
        for j in range(1, b):
            send_tokens(c, j).wait_send()
            for z in range(a):
                pl.when((z == zi) | straight)(lambda: share_copy(c, z, j).wait_send())
                pl.when(straight)(lambda: recv_share(c, z, j).wait_recv())
        for d in range(a):
            pl.when(d != zi)(lambda: pass_sum(0, c, d).wait_send())
        for h in range(a - 1):
            for side, owned, further in ((0, zi >= h, has_right), (1, zi + h < a, has_left)):
                pl.when(owned & further)(lambda: pass_copy(side, c, h, zi, 0).wait_send())
                if wide:
                    @pl.when(owned & further & across_first(c))
                    def _():
                        for j in range(1, b):
                            pass_copy(side, c, h, zi, j).wait_send()
        own_copy(c).wait()
        for k in range(2):
            for j in range(1, m):
                send_flat(c, k, j).wait_send()
                recv_flat(c, k, j).wait_recv()
            own_flat(c, k).wait()


def shards(n, m, patches, cotangent, weight, accum):
    a = 1
    while a * a < n:
        a *= 2
    b = n // a
    nc = 16 if b == 2 else 8
    wide = 4 if b == 2 else 0
    direct = weight.shape[0] % 128 == 0
    tok, dim = patches.shape
    rows, full = weight.shape
    cc = full // nc
    columns = b if wide else 1
    scale = 1.0
    while (2 * scale * largest_product * tok * n) ** power < 2.0 ** 125:
        scale *= 2
    while (scale * largest_product * tok * n) ** power >= 2.0 ** 125:
        scale /= 2
    f32, bf16 = jnp.float32, jnp.bfloat16
    dma = pltpu.SemaphoreType.DMA
    flops = 2 * tok * b * a * rows * full
    return pl.pallas_call(
        functools.partial(kernel, a, b, m, direct, wide, scale),
        out_shape=(
            pltpu.VMEM((rows // m, full * m), f32),
            pltpu.VMEM((rows // m, full * m), f32),
            pltpu.VMEM((dim, full), bf16),
        ),
        in_specs=[pl.BlockSpec(memory_space=pl.ANY)] * 4,
        out_specs=(pl.BlockSpec(memory_space=pltpu.VMEM),) * 3,
        scratch_shapes=[
            pltpu.VMEM((a, b, tok, rows) if direct else (16, 128), bf16),
            pltpu.VMEM((a, rows, b * tok), bf16),
            pltpu.VMEM((nc, b * tok, cc), bf16),
            pltpu.VMEM((nc, rows, cc), f32),
            pltpu.VMEM((nc, rows, cc), f32),
            pltpu.VMEM((nc, rows, cc), bf16),
            pltpu.VMEM((rows, cc), f32),
            pltpu.VMEM((2, nc, a, rows, cc), bf16),
            pltpu.VMEM((nc, a, rows, cc), bf16),
            dma((a,)),
            dma((a, b)),
            dma((a, b)),
            dma((a, b, m)),
            dma((a, b, m)),
            dma((2, nc, b)),
            dma((3, nc)),
            dma((nc, a)),
            dma((2, nc, a)),
            dma((2, nc, a, columns)),
            dma((2, nc, a, columns)),
            dma((nc, a, b)),
            dma((nc, a, b)),
            dma((nc, 2, m)),
            dma((nc, 2, m)),
            dma((nc, 3)),
        ],
        compiler_params=pltpu.CompilerParams(
            collective_id=0, has_side_effects=True, vmem_limit_bytes=48 * 1024 * 1024),
        cost_estimate=pl.CostEstimate(flops=flops, bytes_accessed=4 * dim * full, transcendentals=rows * full),
    )(patches if direct else patches.T, cotangent, weight, accum)


def solution(mesh):
    return jax.shard_map(
        functools.partial(shards, mesh.shape["dp"], mesh.shape["mp"]),
        mesh=mesh,
        in_specs=(P("dp", None), P("dp", "mp"), P("dp", "mp"), P("dp", "mp")),
        out_specs=(P(("dp", "mp"), None), P(("dp", "mp"), None), P(None, "mp")),
        check_vma=False,
    )
```

time: 224 us -> 178 us (0.79)
  Pallas kernels: 217 us -> 172 us
    pallas_call x1, Pallas kernels: 217 us -> 172 us  [shards(): pl.pallas_call(functools.partial(kernel, a, b, m, direct, wide, scale), o...]
where the time goes in v1:
time: 178 us
  Pallas kernels  172 us (97%)
  local copies, waits for them, and re-layouts  6.04 us (3%)
    pallas_call x1, Pallas kernels, shards(): pl.pallas_call(functools.partial(kernel, a, b, m, direct, wide, scale), o...  172 us
    unnamed x3, local copies, waits for them, and re-layouts  6.04 us

profile of v1, /device:TPU:0, one launch (start us, length us, event | category | flops | bytes accessed | tf_op | source)
XLA Modules:
  0.0 178.2 jit_solution(9737085631588993743)
XLA Ops:
  0.6 171.5 %shard_map.67 = (f32[64,8192]{1,0:T(8,128)S(1)}, f32[64,8192]{1,0:T(8,128)S(1)}, bf16[2048,2048]{1,0:T(8,128)(2,1)S(1)}) custom-call(bf16[512,2048]{1,0:T(8,128)(2,1)} %p_ref.1, bf16[512,2048]{1,0:T(8,128)(2,1)} %t_ref.1, f32[256,2048]{1,0:T(8,128)} %w_ref.1, f32[256,2048]{1,0:T(8,128)} %s_ref.1), custom_call_target="tpu_custom_call" | custom-call | flops 4294967296 | bytes 16777216 | tf_op jit(solution)/shard_map/pallas_call | solution.py:369
  172.2 1.3 copy.10
  173.5 1.3 copy.11
  174.8 3.4 %copy.12 = bf16[2048,2048]{1,0:T(8,128)(2,1)} copy(bf16[2048,2048]{1,0:T(8,128)(2,1)S(1)} %get-tuple-element.5) | data formatting | bytes 16777216

commit v2 on v1

v2 whole, which is shorter than its diff:
```python
import functools

import jax
import jax.numpy as jnp
from jax import lax
from jax.experimental import pallas as pl
from jax.experimental.pallas import tpu as pltpu
from jax.sharding import PartitionSpec as P

learning_rate = 0.02
largest_product = 0.5625
power = 7
sum_lag, own_lag, copy_lag, end_lag, cross_lag = 1, 0, 1, 0, 4


def kernel(a, b, m, nc, direct, crossing, scale, p_ref, t_ref, w_ref, s_ref, ow_ref, os_ref, oc_ref,
           pv, pt, tv, wv, sv, gv, rbuf, sbuf,
           fown, fsend, frecv, qsend, qrecv, tsend, trecv, lsem, rsend, rrecv,
           csend, crecv, esend, erecv, osend, xsend, xrecv, yrecv, msend, mrecv):
    rows, full = w_ref.shape
    cc = full // nc
    tok = tv.shape[0] // b
    part_tok = tok // m
    sub = rows // m
    me = lax.axis_index("dp")
    mi = lax.axis_index("mp")
    zi = lax.div(me, b)
    xi = lax.rem(me, b)
    has_left = zi > 0
    has_right = zi < a - 1
    first_cross, step_cross, crossed = crossing

    def inner(j):
        return lax.rem(xi + j, b)

    def peer(j):
        return {"dp": zi * b + inner(j)}

    def other(j):
        return lax.rem(mi + j, m)

    left, right = {"dp": me - b}, {"dp": me + b}

    def remote(src, dst, send, recv, device):
        return pltpu.make_async_remote_copy(
            src_ref=src, dst_ref=dst, send_sem=send, recv_sem=recv,
            device_id=device, device_id_type=pl.DeviceIdType.MESH)

    def span(start, size):
        return pl.ds(pl.multiple_of(start, size), size)

    def cols(c):
        return span(c * cc, cc)

    def block(i):
        return span(i * rows, rows)

    def features(i, q=None):
        toks = slice(None) if q is None else span(q * part_tok, part_tok)
        return p_ref.at[toks, block(i)] if direct else p_ref.at[block(i), toks]

    def gathered(d, x, q=None):
        if direct:
            return pv.at[d, x] if q is None else pv.at[d, x, span(q * part_tok, part_tok)]
        return pt.at[d, :, span(x * tok, tok)] if q is None else pt.at[d, :, span(x * tok + q * part_tok, part_tok)]

    def own_features(d):
        return pltpu.make_async_copy(features(d * b + xi), gathered(d, xi), fown.at[d])

    def send_features(d, j):
        return remote(features(d * b + inner(j), mi), gathered(d, xi, mi), fsend.at[j - 1], frecv.at[d, j - 1], peer(j))

    def recv_features(d, j):
        spot = gathered(d, inner(b - j), mi)
        return remote(spot, spot, fsend.at[j - 1], frecv.at[d, j - 1], peer(j))

    def relay_features(d, j, k):
        spot = gathered(d, inner(b - j), mi)
        return remote(spot, spot, qsend.at[j - 1], qrecv.at[d, j - 1], {"mp": other(k)})

    def relayed(d, j):
        size = (m - 1) * part_tok
        spot = pv.at[d, 0, :size] if direct else pt.at[d, :, :size]
        return remote(spot, spot, qsend.at[j - 1], qrecv.at[d, j - 1], {"mp": other(1)})

    def sent_features(times):
        size = times * part_tok
        return p_ref.at[:size, :a * rows] if direct else p_ref.at[:a * rows, :size]

    def own(k):
        src, dst = ((t_ref, tv.at[span(xi * tok, tok)]), (w_ref, wv), (s_ref, sv))[k]
        return pltpu.make_async_copy(src, dst, lsem.at[k])

    def tokens(c, x):
        return tv.at[span(x * tok, tok), cols(c)]

    def send_tokens(c, j):
        return remote(t_ref.at[:, cols(c)], tokens(c, xi), tsend.at[j - 1], trecv.at[c, j - 1], peer(j))

    def recv_tokens(c, j):
        spot = tokens(c, inner(b - j))
        return remote(spot, spot, tsend.at[j - 1], trecv.at[c, j - 1], peer(j))

    def pass_sum(side, c, d):
        return remote(sbuf.at[c, d], rbuf.at[side, c, d], rsend.at[0], rrecv.at[side, c, d - 1 + side],
                      right if side == 0 else left)

    def region(owner, c):
        return oc_ref.at[block(owner), cols(c)]

    def pass_copy(side, c, h, owner_z):
        spot = region(owner_z * b + xi, c)
        return remote(spot, spot, csend.at[side, h], crecv.at[side, c, h], right if side == 0 else left)

    def pass_crossed(side, c, h, owner_z, j):
        spot = region(owner_z * b + inner(j), c)
        return remote(spot, spot, esend.at[side, h, j - 1], erecv.at[side, cross_index(c), h, j - 1],
                      right if side == 0 else left)

    def own_share(c, j):
        spot = region(me, c)
        return remote(spot, spot, osend.at[j - 1], xrecv.at[zi, j - 1], peer(j))

    def own_cross(c, j):
        spot = region(me, c)
        return remote(spot, spot, osend.at[j - 1], yrecv.at[cross_index(c), j - 1], peer(j))

    def recv_cross(c, j):
        spot = region(zi * b + inner(b - j), c)
        return remote(spot, spot, osend.at[j - 1], yrecv.at[cross_index(c), j - 1], peer(j))

    def share_copy(c, z, j):
        spot = region(z * b + xi, c)
        return remote(spot, spot, xsend.at[z, j - 1], xrecv.at[z, j - 1], peer(j))

    def whole(n, z, send, recv):
        spot = oc_ref.at[block(z * b), :n * cc]
        return remote(spot, spot, send, recv, peer(1))

    def flat(k, device):
        return (ow_ref if k == 0 else os_ref).at[:, span(device * full, full)]

    def flat_chunk(k, device, c):
        return (ow_ref if k == 0 else os_ref).at[:, span(device * full + c * cc, cc)]

    def state(k, i, c):
        return (wv if k == 0 else sv).at[span(i * sub, sub), cols(c)]

    def send_flat(c, k, j):
        return remote(state(k, other(j), c), flat_chunk(k, mi, c), msend.at[k, j - 1], mrecv.at[k, j - 1],
                      {"mp": other(j)})

    def whole_flat(k, j):
        return remote(flat(k, other(m - j)), flat(k, other(m - j)), msend.at[k, j - 1], mrecv.at[k, j - 1],
                      {"mp": other(j)})

    def cross_index(c):
        return lax.div(c - first_cross, step_cross)

    def crosses(c):
        if not crossed:
            return c < 0
        return (c >= first_cross) & (lax.rem(c - first_cross + step_cross * nc, step_cross) == 0) & (
            c < first_cross + step_cross * crossed)

    def valid(c):
        return (c >= 0) & (c < nc)

    barrier = pltpu.get_barrier_semaphore()

    def greet(device):
        pl.semaphore_signal(barrier, inc=1, device_id=device, device_id_type=pl.DeviceIdType.MESH)

    for j in range(1, b):
        greet(peer(j))
    for j in range(1, m):
        greet({"mp": other(j)})
    pl.when(has_left)(lambda: greet(left))
    pl.when(has_right)(lambda: greet(right))

    for d in range(a):
        own_features(d).start()
    for k in range(3):
        own(k).start()

    pl.semaphore_wait(barrier, b - 1 + m - 1 + jnp.minimum(zi, 1) + jnp.minimum(a - 1 - zi, 1))

    ahead = a - 1 - zi
    left_first = zi > ahead

    def nth(k):
        rightward = jnp.where(left_first, k - zi, k)
        leftward = jnp.where(left_first, k, k - ahead)
        goes_left = jnp.where(left_first, k < zi, k >= ahead)
        return jnp.where(k == a - 1, zi, jnp.where(goes_left, leftward, a - 1 - rightward))

    def place(side, k):
        return k + (jnp.where(left_first, zi, 0) if side == 0 else jnp.where(left_first, 0, ahead))

    def start_features(k):
        for j in range(1, b):
            send_features(nth(k), j).start()

    def spread_features(k):
        for j in range(1, b):
            recv_features(nth(k), j).wait_recv()
            for q in range(1, m):
                relay_features(nth(k), j, q).start()

    def start_tokens(c):
        for j in range(1, b):
            send_tokens(c, j).start()

    start_features(0)
    start_tokens(0)
    pl.loop(1, a)(start_features)
    pl.loop(1, nc)(start_tokens)
    spread_features(0)
    own(0).wait()

    def features_here(k, d):
        pl.when(k + 1 < a)(lambda: spread_features(k + 1))
        own_features(d).wait()
        for j in range(1, b):
            relayed(d, j).wait_recv()
        if direct:
            for x in range(b):
                pt[d, :, x * tok:(x + 1) * tok] = pv[d, x].T

    def product(c, d):
        return jnp.dot(pt[d], tv[:, cols(c)], preferred_element_type=jnp.float32)

    def coded(v):
        v = v * scale
        square = v * v
        return (square * square * square * v).astype(jnp.bfloat16)

    def decoded(code):
        c = code.astype(jnp.float32)
        size = jnp.maximum(jnp.abs(c), 2.0 ** -126)
        return c * jnp.exp2(jnp.log2(size) * (1 / power - 1)) * (1 / scale)

    def stage_tokens(c):
        for j in range(1, b):
            recv_tokens(c, j).wait_recv()

    def stage_sums(side, c):
        count, fed = (ahead, has_left) if side == 0 else (zi, has_right)

        @pl.loop(0, count)
        def _(k):
            d = a - 1 - k if side == 0 else k
            pl.when(c == 0)(lambda: features_here(place(side, k), d))

            @pl.when(fed)
            def _():
                total = product(c, d)
                pass_sum(side, c, d).wait_recv()
                sbuf[c, d] = coded(total + decoded(rbuf[side, c, d]))

            @pl.when(jnp.logical_not(fed))
            def _():
                sbuf[c, d] = coded(product(c, d))

            pass_sum(side, c, d).start()

    def stage_update(c):
        @pl.when(c == 0)
        def _():
            features_here(a - 1, zi)
            own(1).wait()
            own(2).wait()

        gv[...] = product(c, zi)
        for side, there in ((0, has_left), (1, has_right)):
            @pl.when(there)
            def _(side=side):
                pass_sum(side, c, zi).wait_recv()
                gv[...] += decoded(rbuf[side, c, zi])
        grad = gv[...]
        summed = sv[:, cols(c)] + grad * grad
        weight = wv[:, cols(c)] - learning_rate * grad * lax.rsqrt(summed)
        oc_ref[block(me), cols(c)] = weight.astype(oc_ref.dtype)
        sv[:, cols(c)] = summed
        wv[:, cols(c)] = weight
        pl.when(has_right)(lambda: pass_copy(0, c, 0, zi).start())
        pl.when(has_left)(lambda: pass_copy(1, c, 0, zi).start())
        for j in range(1, b):
            if crossed:
                pl.when(crosses(c))(lambda: own_cross(c, j).start())
            pl.when(jnp.logical_not(crosses(c)))(lambda: own_share(c, j).start())
        for k in range(2):
            for j in range(1, m):
                send_flat(c, k, j).start()
            flat_chunk(k, mi, c)[...] = state(k, mi, c)[...]

    def stage_across(c):
        for j in range(1, b):
            recv_cross(c, b - j).wait_recv()
            pl.when(has_right)(lambda: pass_crossed(0, c, 0, zi, j).start())
            pl.when(has_left)(lambda: pass_crossed(1, c, 0, zi, j).start())

    def stage_copy(c, side, h, owner_z, further):
        pass_copy(side, c, h - 1, owner_z).wait_recv()
        if further:
            pass_copy(side, c, h, owner_z).start()

        @pl.when(jnp.logical_not(crosses(c)))
        def _():
            for j in range(1, b):
                share_copy(c, owner_z, j).start()

    def stage_crossed(c, side, h, owner_z, further):
        for j in range(1, b):
            pass_crossed(side, c, h - 1, owner_z, j).wait_recv()
            if further:
                pass_crossed(side, c, h, owner_z, j).start()

    def distance(z):
        return jnp.maximum(z, a - 1 - z) * sum_lag + own_lag

    steps = nc + 2 * (a - 1) * max(sum_lag, copy_lag) + own_lag + end_lag + (cross_lag if crossed else 0)

    @pl.loop(0, steps)
    def _(i):
        ready = i - jnp.minimum(zi, a - 1 - zi) * sum_lag
        pl.when(valid(ready))(lambda: stage_tokens(ready))
        going_right = i - zi * sum_lag
        pl.when(valid(going_right))(lambda: stage_sums(0, going_right))
        going_left = i - (a - 1 - zi) * sum_lag
        pl.when(valid(going_left))(lambda: stage_sums(1, going_left))
        mine = i - distance(zi)
        pl.when(valid(mine))(lambda: stage_update(mine))
        if crossed:
            before = mine - cross_lag
            pl.when(valid(before) & crosses(before))(lambda: stage_across(before))
        for h in range(1, a):
            for side in range(2):
                owner_z = zi - h if side == 0 else zi + h
                there = owner_z >= 0 if side == 0 else owner_z < a
                onward = has_right if side == 0 else has_left
                for further in (True, False):
                    here = there & (onward if further else jnp.logical_not(onward))
                    c = i - distance(owner_z) - h * copy_lag - (0 if further else end_lag)
                    pl.when(here & valid(c))(functools.partial(stage_copy, c, side, h, owner_z, further))
                    if crossed:
                        e = c - cross_lag
                        pl.when(here & valid(e) & crosses(e))(
                            functools.partial(stage_crossed, e, side, h, owner_z, further))

    straight = nc - crossed
    for j in range(1, b):
        remote(sent_features(1), sent_features(1), fsend.at[j - 1], frecv.at[0, j - 1], peer(j)).wait_send()
        remote(sent_features(m - 1), sent_features(m - 1), qsend.at[j - 1], frecv.at[0, j - 1], peer(j)).wait_send()
        remote(t_ref, t_ref, tsend.at[j - 1], trecv.at[0, j - 1], peer(j)).wait_send()
        whole(nc, 0, osend.at[j - 1], osend.at[j - 1]).wait_send()
        for z in range(a):
            pl.when(z != zi)(lambda: whole(straight, z, xsend.at[z, j - 1], xrecv.at[z, j - 1]).wait_send())
            whole(straight, z, xsend.at[z, j - 1], xrecv.at[z, j - 1]).wait_recv()
    remote(sbuf.at[:, :a - 1], sbuf.at[:, :a - 1], rsend.at[0], rsend.at[0], peer(1)).wait_send()
    for h in range(a - 1):
        for side, owned, further in ((0, zi >= h, has_right), (1, zi + h < a, has_left)):
            @pl.when(owned & further)
            def _():
                whole(nc, 0, csend.at[side, h], csend.at[side, h]).wait_send()
                if crossed:
                    for j in range(1, b):
                        whole(crossed, 0, esend.at[side, h, j - 1], esend.at[side, h, j - 1]).wait_send()
    for k in range(2):
        for j in range(1, m):
            whole_flat(k, j).wait_send()
            whole_flat(k, j).wait_recv()


def shards(n, m, patches, cotangent, weight, accum):
    a = 1
    while a * a < n:
        a *= 2
    b = n // a
    nc = 16 if b == 2 else 8
    crossing = (1, 2, 2) if b == 2 else (0, 1, 0)
    direct = weight.shape[0] % 128 == 0
    tok, dim = patches.shape
    rows, full = weight.shape
    cc = full // nc
    columns = b - 1 if crossing[2] else 1
    scale = 1.0
    while (2 * scale * largest_product * tok * n) ** power < 2.0 ** 125:
        scale *= 2
    while (scale * largest_product * tok * n) ** power >= 2.0 ** 125:
        scale /= 2
    f32, bf16 = jnp.float32, jnp.bfloat16
    dma = pltpu.SemaphoreType.DMA
    flops = 2 * tok * b * a * rows * full
    return pl.pallas_call(
        functools.partial(kernel, a, b, m, nc, direct, crossing, scale),
        out_shape=(
            pltpu.VMEM((rows // m, full * m), f32),
            pltpu.VMEM((rows // m, full * m), f32),
            pltpu.VMEM((dim, full), bf16),
        ),
        in_specs=[pl.BlockSpec(memory_space=pl.ANY)] * 4,
        out_specs=(pl.BlockSpec(memory_space=pltpu.VMEM),) * 3,
        scratch_shapes=[
            pltpu.VMEM((a, b, tok, rows) if direct else (16, 128), bf16),
            pltpu.VMEM((a, rows, b * tok), bf16),
            pltpu.VMEM((b * tok, full), bf16),
            pltpu.VMEM((rows, full), f32),
            pltpu.VMEM((rows, full), f32),
            pltpu.VMEM((rows, cc), f32),
            pltpu.VMEM((2, nc, a, rows, cc), bf16),
            pltpu.VMEM((nc, a, rows, cc), bf16),
            dma((a,)),
            dma((b - 1,)),
            dma((a, b - 1)),
            dma((b - 1,)),
            dma((a, b - 1)),
            dma((b - 1,)),
            dma((nc, b - 1)),
            dma((3,)),
            dma((1,)),
            dma((2, nc, a - 1)),
            dma((2, a - 1)),
            dma((2, nc, a - 1)),
            dma((2, a - 1, columns)),
            dma((2, max(crossing[2], 1), a - 1, columns)),
            dma((b - 1,)),
            dma((a, b - 1)),
            dma((a, b - 1)),
            dma((max(crossing[2], 1), b - 1)),
            dma((2, m - 1)),
            dma((2, m - 1)),
        ],
        compiler_params=pltpu.CompilerParams(
            collective_id=0, has_side_effects=True, vmem_limit_bytes=48 * 1024 * 1024),
        cost_estimate=pl.CostEstimate(flops=flops, bytes_accessed=4 * dim * full, transcendentals=rows * full),
    )(patches if direct else patches.T, cotangent, weight, accum)


def solution(mesh):
    return jax.shard_map(
        functools.partial(shards, mesh.shape["dp"], mesh.shape["mp"]),
        mesh=mesh,
        in_specs=(P("dp", None), P("dp", "mp"), P("dp", "mp"), P("dp", "mp")),
        out_specs=(P(("dp", "mp"), None), P(("dp", "mp"), None), P(None, "mp")),
        check_vma=False,
    )
```

time: 178 us -> 149 us (0.84)
  Pallas kernels: 172 us -> 142 us
    pallas_call x1, Pallas kernels: 172 us -> 142 us  [shards(): pl.pallas_call(functools.partial(kernel, a, b, m, nc, direct, crossing, s...]
where the time goes in v2:
time: 149 us; the launch traced here: 148 us
  Pallas kernels  142 us (95%)
  local copies, waits for them, and re-layouts  6.04 us (4%)
    pallas_call x1, Pallas kernels, shards(): pl.pallas_call(functools.partial(kernel, a, b, m, nc, direct, crossing, s...  142 us
    unnamed x3, local copies, waits for them, and re-layouts  6.04 us

profile of v2, /device:TPU:0, one launch (start us, length us, event | category | flops | bytes accessed | tf_op | source)
XLA Modules:
  0.0 148.4 jit_solution(8506726189843000255)
XLA Ops:
  0.6 141.8 %shard_map.67 = (f32[64,8192]{1,0:T(8,128)S(1)}, f32[64,8192]{1,0:T(8,128)S(1)}, bf16[2048,2048]{1,0:T(8,128)(2,1)S(1)}) custom-call(bf16[512,2048]{1,0:T(8,128)(2,1)} %p_ref.1, bf16[512,2048]{1,0:T(8,128)(2,1)} %t_ref.1, f32[256,2048]{1,0:T(8,128)} %w_ref.1, f32[256,2048]{1,0:T(8,128)} %s_ref.1), custom_call_target="tpu_custom_call" | custom-call | flops 4294967296 | bytes 16777216 | tf_op jit(solution)/shard_map/pallas_call | solution.py:395
  142.4 1.3 copy.10
  143.7 1.3 copy.11
  145.0 3.4 %copy.12 = bf16[2048,2048]{1,0:T(8,128)(2,1)} copy(bf16[2048,2048]{1,0:T(8,128)(2,1)S(1)} %get-tuple-element.5) | data formatting | bytes 16777216

commit v3 on v2

--- a/solution.py
+++ b/solution.py
@@ -10,12 +10,12 @@
 learning_rate = 0.02
 largest_product = 0.5625
 power = 7
-sum_lag, own_lag, copy_lag, end_lag, cross_lag = 1, 0, 1, 0, 4
+sum_lag, own_lag, copy_lag, end_lag, cross_lag, token_lead = 1, 0, 1, 3, 3, 6
 
 
 def kernel(a, b, m, nc, direct, crossing, scale, p_ref, t_ref, w_ref, s_ref, ow_ref, os_ref, oc_ref,
            pv, pt, tv, wv, sv, gv, rbuf, sbuf,
-           fown, fsend, frecv, qsend, qrecv, tsend, trecv, lsem, rsend, rrecv,
+           fown, fsend, frecv, qsend, qrecv, grecv, tsend, trecv, lsem, rsend, rrecv,
            csend, crecv, esend, erecv, osend, xsend, xrecv, yrecv, msend, mrecv):
     rows, full = w_ref.shape
     cc = full // nc
@@ -28,7 +28,11 @@
     xi = lax.rem(me, b)
     has_left = zi > 0
     has_right = zi < a - 1
-    first_cross, step_cross, crossed = crossing
+    crossed = len(crossing[0] + crossing[1]) > 0
+    cores = 2 if m % 2 == 0 else 1
+    pairs = m // cores
+    pair = lax.div(mi, cores)
+    core = lax.rem(mi, cores)
 
     def inner(j):
         return lax.rem(xi + j, b)
@@ -74,14 +78,28 @@
         spot = gathered(d, inner(b - j), mi)
         return remote(spot, spot, fsend.at[j - 1], frecv.at[d, j - 1], peer(j))
 
+    def mate(k):
+        return pair * cores + lax.rem(core + k, cores)
+
+    def across_pairs(k):
+        return lax.rem(pair + k, pairs) * cores + core
+
     def relay_features(d, j, k):
         spot = gathered(d, inner(b - j), mi)
-        return remote(spot, spot, qsend.at[j - 1], qrecv.at[d, j - 1], {"mp": other(k)})
-
-    def relayed(d, j):
-        size = (m - 1) * part_tok
+        return remote(spot, spot, qsend.at[j - 1], grecv.at[d, j - 1, k - 1], {"mp": across_pairs(k)})
+
+    def recv_relay(d, j, k):
+        spot = gathered(d, inner(b - j), across_pairs(pairs - k))
+        return remote(spot, spot, qsend.at[j - 1], grecv.at[d, j - 1, k - 1], {"mp": across_pairs(k)})
+
+    def hand_features(d, j, k, q):
+        spot = gathered(d, inner(b - j), q)
+        return remote(spot, spot, qsend.at[j - 1], qrecv.at[d, j - 1], {"mp": mate(k)})
+
+    def handed(d, j):
+        size = (cores - 1) * pairs * part_tok
         spot = pv.at[d, 0, :size] if direct else pt.at[d, :, :size]
-        return remote(spot, spot, qsend.at[j - 1], qrecv.at[d, j - 1], {"mp": other(1)})
+        return remote(spot, spot, qsend.at[j - 1], qrecv.at[d, j - 1], {"mp": mate(1)})
 
     def sent_features(times):
         size = times * part_tok
@@ -114,7 +132,7 @@
 
     def pass_crossed(side, c, h, owner_z, j):
         spot = region(owner_z * b + inner(j), c)
-        return remote(spot, spot, esend.at[side, h, j - 1], erecv.at[side, cross_index(c), h, j - 1],
+        return remote(spot, spot, esend.at[side, h, j - 1], erecv.at[side, c, h, j - 1],
                       right if side == 0 else left)
 
     def own_share(c, j):
@@ -123,11 +141,11 @@
 
     def own_cross(c, j):
         spot = region(me, c)
-        return remote(spot, spot, osend.at[j - 1], yrecv.at[cross_index(c), j - 1], peer(j))
+        return remote(spot, spot, osend.at[j - 1], yrecv.at[c, j - 1], peer(j))
 
     def recv_cross(c, j):
         spot = region(zi * b + inner(b - j), c)
-        return remote(spot, spot, osend.at[j - 1], yrecv.at[cross_index(c), j - 1], peer(j))
+        return remote(spot, spot, osend.at[j - 1], yrecv.at[c, j - 1], peer(j))
 
     def share_copy(c, z, j):
         spot = region(z * b + xi, c)
@@ -154,14 +172,13 @@
         return remote(flat(k, other(m - j)), flat(k, other(m - j)), msend.at[k, j - 1], mrecv.at[k, j - 1],
                       {"mp": other(j)})
 
-    def cross_index(c):
-        return lax.div(c - first_cross, step_cross)
-
-    def crosses(c):
-        if not crossed:
-            return c < 0
-        return (c >= first_cross) & (lax.rem(c - first_cross + step_cross * nc, step_cross) == 0) & (
-            c < first_cross + step_cross * crossed)
+    def at_end(z):
+        return (z == 0) | (z == a - 1)
+
+    masks = [sum(2 ** c for c in chosen) for chosen in crossing]
+
+    def crosses(c, z):
+        return lax.shift_right_logical(jnp.where(at_end(z), masks[0], masks[1]), c) % 2 == 1
 
     def valid(c):
         return (c >= 0) & (c < nc)
@@ -204,8 +221,17 @@
     def spread_features(k):
         for j in range(1, b):
             recv_features(nth(k), j).wait_recv()
-            for q in range(1, m):
+            for q in range(1, pairs):
                 relay_features(nth(k), j, q).start()
+            for q in range(1, cores):
+                hand_features(nth(k), j, q, mi).start()
+
+    def hand_on_features(k):
+        for j in range(1, b):
+            for q in range(1, pairs):
+                recv_relay(nth(k), j, q).wait_recv()
+                for r in range(1, cores):
+                    hand_features(nth(k), j, r, across_pairs(pairs - q)).start()
 
     def start_tokens(c):
         for j in range(1, b):
@@ -214,18 +240,25 @@
     start_features(0)
     start_tokens(0)
     pl.loop(1, a)(start_features)
-    pl.loop(1, nc)(start_tokens)
+    pl.loop(1, min(token_lead, nc))(start_tokens)
     spread_features(0)
+    hand_on_features(0)
+    if a > 1:
+        spread_features(1)
     own(0).wait()
 
-    def features_here(k, d):
-        pl.when(k + 1 < a)(lambda: spread_features(k + 1))
+    def features_here(d):
         own_features(d).wait()
-        for j in range(1, b):
-            relayed(d, j).wait_recv()
+        if cores > 1:
+            for j in range(1, b):
+                handed(d, j).wait_recv()
         if direct:
             for x in range(b):
                 pt[d, :, x * tok:(x + 1) * tok] = pv[d, x].T
+
+    def fetch_features(k):
+        pl.when(k + 2 < a)(lambda: spread_features(k + 2))
+        pl.when(k + 1 < a)(lambda: hand_on_features(k + 1))
 
     def product(c, d):
         return jnp.dot(pt[d], tv[:, cols(c)], preferred_element_type=jnp.float32)
@@ -241,6 +274,7 @@
         return c * jnp.exp2(jnp.log2(size) * (1 / power - 1)) * (1 / scale)
 
     def stage_tokens(c):
+        pl.when(c + token_lead < nc)(lambda: start_tokens(c + token_lead))
         for j in range(1, b):
             recv_tokens(c, j).wait_recv()
 
@@ -250,11 +284,12 @@
         @pl.loop(0, count)
         def _(k):
             d = a - 1 - k if side == 0 else k
-            pl.when(c == 0)(lambda: features_here(place(side, k), d))
+            pl.when(c == 0)(lambda: features_here(d))
 
             @pl.when(fed)
             def _():
                 total = product(c, d)
+                pl.when(c == 0)(lambda: fetch_features(place(side, k)))
                 pass_sum(side, c, d).wait_recv()
                 sbuf[c, d] = coded(total + decoded(rbuf[side, c, d]))
 
@@ -263,11 +298,12 @@
                 sbuf[c, d] = coded(product(c, d))
 
             pass_sum(side, c, d).start()
+            pl.when((c == 0) & jnp.logical_not(fed))(lambda: fetch_features(place(side, k)))
 
     def stage_update(c):
         @pl.when(c == 0)
         def _():
-            features_here(a - 1, zi)
+            features_here(zi)
             own(1).wait()
             own(2).wait()
 
@@ -287,8 +323,8 @@
         pl.when(has_left)(lambda: pass_copy(1, c, 0, zi).start())
         for j in range(1, b):
             if crossed:
-                pl.when(crosses(c))(lambda: own_cross(c, j).start())
-            pl.when(jnp.logical_not(crosses(c)))(lambda: own_share(c, j).start())
+                pl.when(crosses(c, zi))(lambda: own_cross(c, j).start())
+            pl.when(jnp.logical_not(crosses(c, zi)))(lambda: own_share(c, j).start())
         for k in range(2):
             for j in range(1, m):
                 send_flat(c, k, j).start()
@@ -305,7 +341,7 @@
         if further:
             pass_copy(side, c, h, owner_z).start()
 
-        @pl.when(jnp.logical_not(crosses(c)))
+        @pl.when(jnp.logical_not(crosses(c, owner_z)))
         def _():
             for j in range(1, b):
                 share_copy(c, owner_z, j).start()
@@ -333,7 +369,12 @@
         pl.when(valid(mine))(lambda: stage_update(mine))
         if crossed:
             before = mine - cross_lag
-            pl.when(valid(before) & crosses(before))(lambda: stage_across(before))
+
+            @pl.when(valid(before))
+            def _():
+                pl.when(crosses(before, zi))(lambda: stage_across(before))
+
+
         for h in range(1, a):
             for side in range(2):
                 owner_z = zi - h if side == 0 else zi + h
@@ -345,31 +386,64 @@
                     pl.when(here & valid(c))(functools.partial(stage_copy, c, side, h, owner_z, further))
                     if crossed:
                         e = c - cross_lag
-                        pl.when(here & valid(e) & crosses(e))(
-                            functools.partial(stage_crossed, e, side, h, owner_z, further))
-
-    straight = nc - crossed
+
+                        @pl.when(here & valid(e))
+                        def _(e=e, side=side, h=h, owner_z=owner_z, further=further):
+                            pl.when(crosses(e, owner_z))(
+                                lambda: stage_crossed(e, side, h, owner_z, further))
+
     for j in range(1, b):
         remote(sent_features(1), sent_features(1), fsend.at[j - 1], frecv.at[0, j - 1], peer(j)).wait_send()
         remote(sent_features(m - 1), sent_features(m - 1), qsend.at[j - 1], frecv.at[0, j - 1], peer(j)).wait_send()
         remote(t_ref, t_ref, tsend.at[j - 1], trecv.at[0, j - 1], peer(j)).wait_send()
         whole(nc, 0, osend.at[j - 1], osend.at[j - 1]).wait_send()
         for z in range(a):
+            straight = nc - len(crossing[0 if z in (0, a - 1) else 1])
             pl.when(z != zi)(lambda: whole(straight, z, xsend.at[z, j - 1], xrecv.at[z, j - 1]).wait_send())
             whole(straight, z, xsend.at[z, j - 1], xrecv.at[z, j - 1]).wait_recv()
     remote(sbuf.at[:, :a - 1], sbuf.at[:, :a - 1], rsend.at[0], rsend.at[0], peer(1)).wait_send()
     for h in range(a - 1):
-        for side, owned, further in ((0, zi >= h, has_right), (1, zi + h < a, has_left)):
-            @pl.when(owned & further)
-            def _():
-                whole(nc, 0, csend.at[side, h], csend.at[side, h]).wait_send()
-                if crossed:
-                    for j in range(1, b):
-                        whole(crossed, 0, esend.at[side, h, j - 1], esend.at[side, h, j - 1]).wait_send()
+        for side, owner_z, onward in ((0, zi - h, has_right), (1, zi + h, has_left)):
+            sent = onward & (owner_z >= 0) & (owner_z < a)
+            pl.when(sent)(lambda: whole(nc, 0, csend.at[side, h], csend.at[side, h]).wait_send())
+            for chosen, there in ((crossing[0], at_end(owner_z)), (crossing[1], jnp.logical_not(at_end(owner_z)))):
+                if chosen:
+                    @pl.when(sent & there)
+                    def _():
+                        for j in range(1, b):
+                            spot = esend.at[side, h, j - 1]
+                            whole(len(chosen), 0, spot, spot).wait_send()
     for k in range(2):
         for j in range(1, m):
             whole_flat(k, j).wait_send()
             whole_flat(k, j).wait_recv()
+
+
+def leave(pieces, *refs):
+    count = len(refs) // 2
+    sems = refs[-1]
+    copies = []
+    for k, (src, dst) in enumerate(zip(refs[:count], refs[count:2 * count])):
+        step = src.shape[0] // pieces
+        for i in range(pieces):
+            part = slice(i * step, (i + 1) * step)
+            copies.append(pltpu.make_async_copy(src.at[part], dst.at[part], sems.at[k, i]))
+    for copy in copies:
+        copy.start()
+    for copy in copies:
+        copy.wait()
+
+
+def placed(results):
+    pieces = 4
+    return pl.pallas_call(
+        functools.partial(leave, pieces),
+        out_shape=tuple(jax.ShapeDtypeStruct(r.shape, r.dtype) for r in results),
+        in_specs=[pl.BlockSpec(memory_space=pltpu.VMEM)] * len(results),
+        out_specs=(pl.BlockSpec(memory_space=pl.ANY),) * len(results),
+        scratch_shapes=[pltpu.SemaphoreType.DMA((len(results), pieces))],
+        compiler_params=pltpu.CompilerParams(vmem_limit_bytes=20 * 1024 * 1024),
+    )(*results)
 
 
 def shards(n, m, patches, cotangent, weight, accum):
@@ -378,12 +452,14 @@
         a *= 2
     b = n // a
     nc = 16 if b == 2 else 8
-    crossing = (1, 2, 2) if b == 2 else (0, 1, 0)
+    crossing = ((7, 9, 10, 11, 12, 15), (2, 15)) if b == 2 else ((), ())
+    crossed = len(crossing[0] + crossing[1]) > 0
+    pairs = m // 2 if m % 2 == 0 else m
     direct = weight.shape[0] % 128 == 0
     tok, dim = patches.shape
     rows, full = weight.shape
     cc = full // nc
-    columns = b - 1 if crossing[2] else 1
+    columns = b - 1 if crossing[0] + crossing[1] else 1
     scale = 1.0
     while (2 * scale * largest_product * tok * n) ** power < 2.0 ** 125:
         scale *= 2
@@ -392,7 +468,7 @@
     f32, bf16 = jnp.float32, jnp.bfloat16
     dma = pltpu.SemaphoreType.DMA
     flops = 2 * tok * b * a * rows * full
-    return pl.pallas_call(
+    results = pl.pallas_call(
         functools.partial(kernel, a, b, m, nc, direct, crossing, scale),
         out_shape=(
             pltpu.VMEM((rows // m, full * m), f32),
@@ -415,6 +491,7 @@
             dma((a, b - 1)),
             dma((b - 1,)),
             dma((a, b - 1)),
+            dma((a, b - 1, max(pairs - 1, 1))),
             dma((b - 1,)),
             dma((nc, b - 1)),
             dma((3,)),
@@ -423,11 +500,11 @@
             dma((2, a - 1)),
             dma((2, nc, a - 1)),
             dma((2, a - 1, columns)),
-            dma((2, max(crossing[2], 1), a - 1, columns)),
+            dma((2, nc if crossed else 1, a - 1, columns)),
             dma((b - 1,)),
             dma((a, b - 1)),
             dma((a, b - 1)),
-            dma((max(crossing[2], 1), b - 1)),
+            dma((nc if crossed else 1, b - 1)),
             dma((2, m - 1)),
             dma((2, m - 1)),
         ],
@@ -435,6 +512,7 @@
             collective_id=0, has_side_effects=True, vmem_limit_bytes=48 * 1024 * 1024),
         cost_estimate=pl.CostEstimate(flops=flops, bytes_accessed=4 * dim * full, transcendentals=rows * full),
     )(patches if direct else patches.T, cotangent, weight, accum)
+    return placed(results)
 
 
 def solution(mesh):

time: 149 us -> 143 us (0.960)
  local copies, waits for them, and re-layouts: 6.04 us -> 0 us
    unnamed x3 -> x0, local copies, waits for them, and re-layouts: 6.04 us -> none
    pallas_call x0 -> x1, Pallas kernels: none -> 4.7 us  [placed(): pl.pallas_call(functools.partial(leave, pieces), out_shape=tuple((jax.Sha...]
    pallas_call x1, Pallas kernels: 142 us -> 138 us  [shards(): pl.pallas_call(functools.partial(kernel, a, b, m, nc, direct, crossing, s...]
where the time goes in v3:
time: 143 us
  Pallas kernels  143 us (100%)
    pallas_call x1, Pallas kernels, shards(): pl.pallas_call(functools.partial(kernel, a, b, m, nc, direct, crossing, s...  138 us
    pallas_call x1, Pallas kernels, placed(): pl.pallas_call(functools.partial(leave, pieces), out_shape=tuple((jax.Sha...  4.7 us

profile of v3, /device:TPU:0, one launch (start us, length us, event | category | flops | bytes accessed | tf_op | source)
XLA Modules:
  0.0 143.3 jit_solution(808436870798153628)
XLA Ops:
  0.6 137.9 %shard_map.67 = (f32[64,8192]{1,0:T(8,128)S(1)}, f32[64,8192]{1,0:T(8,128)S(1)}, bf16[2048,2048]{1,0:T(8,128)(2,1)S(1)}) custom-call(bf16[512,2048]{1,0:T(8,128)(2,1)} %p_ref.1, bf16[512,2048]{1,0:T(8,128)(2,1)} %t_ref.1, f32[256,2048]{1,0:T(8,128)} %w_ref.1, f32[256,2048]{1,0:T(8,128)} %s_ref.1), custom_call_target="tpu_custom_call" | custom-call | flops 4294967296 | bytes 16777216 | tf_op jit(solution)/shard_map/pallas_call | solution.py:471
  138.6 4.7 %shard_map.68 = (f32[64,8192]{1,0:T(8,128)}, f32[64,8192]{1,0:T(8,128)}, bf16[2048,2048]{1,0:T(8,128)(2,1)}) custom-call(f32[64,8192]{1,0:T(8,128)S(1)} %get-tuple-element.6.refs_0_, f32[64,8192]{1,0:T(8,128)S(1)} %get-tuple-element.7.refs_1_, bf16[2048,2048]{1,0:T(8,128)(2,1)S(1)} %get-tuple-element.8.refs_2_), custom_call_target="tpu_custom_call" | custom-call | tf_op jit(solution)/shard_map/pallas_call | solution.py:439

commit v4 on v3

--- a/solution.py
+++ b/solution.py
@@ -120,7 +120,7 @@
         return remote(spot, spot, tsend.at[j - 1], trecv.at[c, j - 1], peer(j))
 
     def pass_sum(side, c, d):
-        return remote(sbuf.at[c, d], rbuf.at[side, c, d], rsend.at[0], rrecv.at[side, c, d - 1 + side],
+        return remote(sbuf.at[c, d], rbuf.at[side, c, d], rsend.at[0], rrecv.at[c, d + 1 - side],
                       right if side == 0 else left)
 
     def region(owner, c):
@@ -128,11 +128,11 @@
 
     def pass_copy(side, c, h, owner_z):
         spot = region(owner_z * b + xi, c)
-        return remote(spot, spot, csend.at[side, h], crecv.at[side, c, h], right if side == 0 else left)
+        return remote(spot, spot, csend.at[side, h], crecv.at[c, owner_z - side], right if side == 0 else left)
 
     def pass_crossed(side, c, h, owner_z, j):
         spot = region(owner_z * b + inner(j), c)
-        return remote(spot, spot, esend.at[side, h, j - 1], erecv.at[side, c, h, j - 1],
+        return remote(spot, spot, esend.at[side, h, j - 1], erecv.at[c, owner_z - side, j - 1],
                       right if side == 0 else left)
 
     def own_share(c, j):
@@ -362,9 +362,11 @@
         ready = i - jnp.minimum(zi, a - 1 - zi) * sum_lag
         pl.when(valid(ready))(lambda: stage_tokens(ready))
         going_right = i - zi * sum_lag
+        going_left = i - (a - 1 - zi) * sum_lag
+        early = jnp.logical_not(left_first)
+        pl.when(valid(going_left) & early)(lambda: stage_sums(1, going_left))
         pl.when(valid(going_right))(lambda: stage_sums(0, going_right))
-        going_left = i - (a - 1 - zi) * sum_lag
-        pl.when(valid(going_left))(lambda: stage_sums(1, going_left))
+        pl.when(valid(going_left) & jnp.logical_not(early))(lambda: stage_sums(1, going_left))
         mine = i - distance(zi)
         pl.when(valid(mine))(lambda: stage_update(mine))
         if crossed:
@@ -496,11 +498,11 @@
             dma((nc, b - 1)),
             dma((3,)),
             dma((1,)),
-            dma((2, nc, a - 1)),
+            dma((nc, a + 1)),
             dma((2, a - 1)),
-            dma((2, nc, a - 1)),
+            dma((nc, a - 1)),
             dma((2, a - 1, columns)),
-            dma((2, nc if crossed else 1, a - 1, columns)),
+            dma((nc if crossed else 1, a - 1, columns)),
             dma((b - 1,)),
             dma((a, b - 1)),
             dma((a, b - 1)),

time: 143 us -> 142 us (level)
  Pallas kernels: 143 us -> 141 us
    pallas_call x1, Pallas kernels: 138 us -> 136 us  [shards(): pl.pallas_call(functools.partial(kernel, a, b, m, nc, direct, crossing, s...]
where the time goes in v4:
time: 142 us
  Pallas kernels  141 us (99%)
    pallas_call x1, Pallas kernels, shards(): pl.pallas_call(functools.partial(kernel, a, b, m, nc, direct, crossing, s...  136 us
    pallas_call x1, Pallas kernels, placed(): pl.pallas_call(functools.partial(leave, pieces), out_shape=tuple((jax.Sha...  4.7 us

profile of v4, /device:TPU:0, one launch (start us, length us, event | category | flops | bytes accessed | tf_op | source)
XLA Modules:
  0.0 141.7 jit_solution(6291681844774644145)
XLA Ops:
  0.6 136.3 %shard_map.67 = (f32[64,8192]{1,0:T(8,128)S(1)}, f32[64,8192]{1,0:T(8,128)S(1)}, bf16[2048,2048]{1,0:T(8,128)(2,1)S(1)}) custom-call(bf16[512,2048]{1,0:T(8,128)(2,1)} %p_ref.1, bf16[512,2048]{1,0:T(8,128)(2,1)} %t_ref.1, f32[256,2048]{1,0:T(8,128)} %w_ref.1, f32[256,2048]{1,0:T(8,128)} %s_ref.1), custom_call_target="tpu_custom_call" | custom-call | flops 4294967296 | bytes 16777216 | tf_op jit(solution)/shard_map/pallas_call | solution.py:473
  137.0 4.7 %shard_map.68 = (f32[64,8192]{1,0:T(8,128)}, f32[64,8192]{1,0:T(8,128)}, bf16[2048,2048]{1,0:T(8,128)(2,1)}) custom-call(f32[64,8192]{1,0:T(8,128)S(1)} %get-tuple-element.6.refs_0_, f32[64,8192]{1,0:T(8,128)S(1)} %get-tuple-element.7.refs_1_, bf16[2048,2048]{1,0:T(8,128)(2,1)S(1)} %get-tuple-element.8.refs_2_), custom_call_target="tpu_custom_call" | custom-call | tf_op jit(solution)/shard_map/pallas_call | solution.py:441

commit v5 on v4

--- a/solution.py
+++ b/solution.py
@@ -10,7 +10,7 @@
 learning_rate = 0.02
 largest_product = 0.5625
 power = 7
-sum_lag, own_lag, copy_lag, end_lag, cross_lag, token_lead = 1, 0, 1, 3, 3, 6
+sum_lag, own_lag, copy_lag, end_lag, cross_lag, token_lead = 1, 0, 1, 2, 6, 9
 
 
 def kernel(a, b, m, nc, direct, crossing, scale, p_ref, t_ref, w_ref, s_ref, ow_ref, os_ref, oc_ref,
@@ -132,7 +132,7 @@
 
     def pass_crossed(side, c, h, owner_z, j):
         spot = region(owner_z * b + inner(j), c)
-        return remote(spot, spot, esend.at[side, h, j - 1], erecv.at[c, owner_z - side, j - 1],
+        return remote(spot, spot, esend.at[side, h, j - 1], erecv.at[rank(c), owner_z - side, j - 1],
                       right if side == 0 else left)
 
     def own_share(c, j):
@@ -141,11 +141,11 @@
 
     def own_cross(c, j):
         spot = region(me, c)
-        return remote(spot, spot, osend.at[j - 1], yrecv.at[c, j - 1], peer(j))
+        return remote(spot, spot, osend.at[j - 1], yrecv.at[rank(c), j - 1], peer(j))
 
     def recv_cross(c, j):
         spot = region(zi * b + inner(b - j), c)
-        return remote(spot, spot, osend.at[j - 1], yrecv.at[c, j - 1], peer(j))
+        return remote(spot, spot, osend.at[j - 1], yrecv.at[rank(c), j - 1], peer(j))
 
     def share_copy(c, z, j):
         spot = region(z * b + xi, c)
@@ -179,6 +179,9 @@
 
     def crosses(c, z):
         return lax.shift_right_logical(jnp.where(at_end(z), masks[0], masks[1]), c) % 2 == 1
+
+    def rank(c):
+        return sum((jnp.where(c > q, 1, 0) for q in sorted(set(crossing[0] + crossing[1]))), 0)
 
     def valid(c):
         return (c >= 0) & (c < nc)
@@ -454,8 +457,8 @@
         a *= 2
     b = n // a
     nc = 16 if b == 2 else 8
-    crossing = ((7, 9, 10, 11, 12, 15), (2, 15)) if b == 2 else ((), ())
-    crossed = len(crossing[0] + crossing[1]) > 0
+    crossing = ((4, 6, 8, 9, 10, 12), (6, 11)) if b == 2 else ((), ())
+    crossed = len(set(crossing[0] + crossing[1]))
     pairs = m // 2 if m % 2 == 0 else m
     direct = weight.shape[0] % 128 == 0
     tok, dim = patches.shape
@@ -502,11 +505,11 @@
             dma((2, a - 1)),
             dma((nc, a - 1)),
             dma((2, a - 1, columns)),
-            dma((nc if crossed else 1, a - 1, columns)),
+            dma((max(crossed, 1), a - 1, columns)),
             dma((b - 1,)),
             dma((a, b - 1)),
             dma((a, b - 1)),
-            dma((nc if crossed else 1, b - 1)),
+            dma((max(crossed, 1), b - 1)),
             dma((2, m - 1)),
             dma((2, m - 1)),
         ],

time: 142 us -> 141 us (level)
  no operation moved by 1% of the time
where the time goes in v5:
time: 141 us
  Pallas kernels  141 us (100%)
    pallas_call x1, Pallas kernels, shards(): pl.pallas_call(functools.partial(kernel, a, b, m, nc, direct, crossing, s...  136 us
    pallas_call x1, Pallas kernels, placed(): pl.pallas_call(functools.partial(leave, pieces), out_shape=tuple((jax.Sha...  4.7 us

profile of v5, /device:TPU:0, one launch (start us, length us, event | category | flops | bytes accessed | tf_op | source)
XLA Modules:
  0.0 141.3 jit_solution(12191075234967906126)
XLA Ops:
  0.6 136.0 %shard_map.67 = (f32[64,8192]{1,0:T(8,128)S(1)}, f32[64,8192]{1,0:T(8,128)S(1)}, bf16[2048,2048]{1,0:T(8,128)(2,1)S(1)}) custom-call(bf16[512,2048]{1,0:T(8,128)(2,1)} %p_ref.1, bf16[512,2048]{1,0:T(8,128)(2,1)} %t_ref.1, f32[256,2048]{1,0:T(8,128)} %w_ref.1, f32[256,2048]{1,0:T(8,128)} %s_ref.1), custom_call_target="tpu_custom_call" | custom-call | flops 4294967296 | bytes 16777216 | tf_op jit(solution)/shard_map/pallas_call | solution.py:476
  136.6 4.7 %shard_map.68 = (f32[64,8192]{1,0:T(8,128)}, f32[64,8192]{1,0:T(8,128)}, bf16[2048,2048]{1,0:T(8,128)(2,1)}) custom-call(f32[64,8192]{1,0:T(8,128)S(1)} %get-tuple-element.6.refs_0_, f32[64,8192]{1,0:T(8,128)S(1)} %get-tuple-element.7.refs_1_, bf16[2048,2048]{1,0:T(8,128)(2,1)S(1)} %get-tuple-element.8.refs_2_), custom_call_target="tpu_custom_call" | custom-call | tf_op jit(solution)/shard_map/pallas_call | solution.py:444
